TPU v7x, 32 devices: a whole 2x2x4 slice. The times are simulated.
32 devices in a mesh: space: 16 (over z, y, core), lat: 2 (over x).
Axes of the slice: x: 2, y: 2, z: 4, core: 2. Of those that a mesh axis runs over, the one named last changes fastest.
Arguments:
- fields: bfloat16 [4, 64, 3, 65536], P(None, None, None, ('space', 'lat')), may hold values from -6 to 6
- cell_latent: int32 [65536], P(('space', 'lat')), may hold values from 0 to 1023, as said below
- enc_weight: float32 [3, 65536], P(None, ('space', 'lat')), may hold values from -0.4375 to 0.4375
- dec_weight: float32 [3, 65536], P(None, ('space', 'lat')), may hold values from -5 to 5
- trans_weight: bfloat16 [1024, 64, 5120], P(('space', 'lat')), may hold values from -0.15625 to 0.15625
- graph_logits: float32 [1024, 5120], P(('space', 'lat')), may hold values from -6 to 6
- hidden_bias: float32 [1024, 64], P(('space', 'lat')), may hold values from -3 to 3
- out_weight: float32 [1024, 64], P(('space', 'lat')), may hold values from -0.75 to 0.75
- noise_var: float32 [1024], P(('space', 'lat')), may hold values from 0.005 to 0.05
Outputs:
- grad_enc: float32 [3, 65536], P(None, ('space', 'lat'))
- grad_dec: float32 [3, 65536], P(None, ('space', 'lat'))
- grad_trans: bfloat16 [1024, 64, 5120], P(('space', 'lat'))
- grad_graph: float32 [1024, 5120], P(('space', 'lat'))
Inputs may be any that keep to these rules, and one draw needn't show every extreme that they name: `cell_latent`: cells d * 2048 to (d + 1) * 2048 - 1 are assigned latents from (d - 1) * 32 to (d + 2) * 32 - 1; for every d other than the first, the first of these cells has a latent below d * 32, and for every d other than the last, the last has one at (d + 1) * 32 or above.
All inputs are finite; a program needn't handle non-finite values.
Results may differ from a plain program's by a relative error of at most 0.0023.
The roundings to bfloat16 on the way count: a program that leaves them out, or rounds other values in their place, can miss the bound.
Values may be sent and summed in bfloat16 or wider, within the bound.
No kernel may reach another device: no remote copies, remote signals or barrier semaphores. Data moves between devices by JAX's collectives and lax.ppermute only.
A program may use at most 192 MiB of HBM per device.

v0:
```python
import jax
import jax.numpy as jnp
from jax import lax
from jax.sharding import PartitionSpec as P

LAGS = 5
sparsity_weight = 0.01


def shifted(block, axis, distance):
    devices = range(lax.axis_size(axis))
    route = [(i - distance, i) for i in devices if i - distance in devices]
    return lax.ppermute(block, axis, route)


def extended(block, sides, width):
    for axis, dim in sides:
        count = lax.axis_size(axis)
        forward = [(i, i + 1) for i in range(count - 1)]
        backward = [(target, source) for source, target in forward]
        low = lax.ppermute(
            lax.slice_in_dim(block, block.shape[dim] - width, None, axis=dim), axis, forward
        )
        high = lax.ppermute(lax.slice_in_dim(block, 0, width, axis=dim), axis, backward)
        block = jnp.concatenate([low, block, high], axis=dim)
    return block


def body(
    fields,
    cell_latent,
    enc_weight,
    dec_weight,
    trans_weight,
    graph_logits,
    hidden_bias,
    out_weight,
    noise_var,
):
    batch_size, step_count, var_count, cell_count = fields.shape
    lat_dev, hidden, lag_width = trans_weight.shape
    latent_count = lag_width // LAGS
    highest = lax.Precision.HIGHEST
    device = lax.axis_index(("space", "lat"))
    norm_factor = 1.0 / (batch_size * step_count)
    rows = batch_size * (step_count - LAGS)
    local_index = cell_latent - (device - 1) * lat_dev
    one_hot = (local_index[:, None] == jnp.arange(3 * lat_dev, dtype=jnp.int32)[None, :]).astype(
        jnp.float32
    )
    projected = jnp.sum(fields.astype(jnp.float32) * enc_weight[None, None], axis=2)
    enc_part = jnp.einsum("btc,cj->btj", projected, one_hot, precision=highest)
    spread_table = jnp.zeros((batch_size, step_count, latent_count + 2 * lat_dev), jnp.float32)
    spread_table = lax.dynamic_update_slice_in_dim(spread_table, enc_part, device * lat_dev, 2)
    latent_full = lax.psum(spread_table[:, :, lat_dev : latent_count + lat_dev], ("space", "lat"))
    own_latent = lax.dynamic_slice_in_dim(latent_full, device * lat_dev, lat_dev, 2)
    latent_bf = latent_full.astype(jnp.bfloat16)
    padded_latent = jnp.pad(latent_bf, ((0, 0), (0, 0), (lat_dev, lat_dev)))
    window = lax.dynamic_slice_in_dim(padded_latent, device * lat_dev, 3 * lat_dev, 2)
    cell_values = jnp.einsum("btj,cj->btc", window.astype(jnp.float32), one_hot, precision=highest)
    resid = dec_weight[None, None] * cell_values[:, :, None, :] - fields.astype(jnp.float32)
    grad_dec = norm_factor * jnp.einsum("btvc,btc->vc", resid, cell_values, precision=highest)
    cell_grad = norm_factor * jnp.sum(resid * dec_weight[None, None], axis=2)
    window_grad = jnp.einsum("btc,cj->btj", cell_grad, one_hot, precision=highest)
    lagged = jnp.stack(
        [latent_bf[:, LAGS - lag : step_count - lag, :] for lag in range(1, LAGS + 1)], axis=2
    )
    lagged = lagged.reshape(rows, lag_width)
    edge_prob = jax.nn.sigmoid(graph_logits)
    eff_weight = (trans_weight.astype(jnp.float32) * edge_prob[:, None, :]).astype(jnp.bfloat16)
    pre_act = (
        jnp.einsum("ri,kmi->rkm", lagged, eff_weight, preferred_element_type=jnp.float32)
        + hidden_bias[None]
    )
    gate_sig = jax.nn.sigmoid(pre_act)
    predicted = jnp.sum(pre_act * gate_sig * out_weight[None], axis=2)
    target = own_latent[:, LAGS:, :].reshape(rows, lat_dev)
    direct = norm_factor * (target - predicted) / noise_var[None]
    hidden_grad = (
        (-direct)[:, :, None] * out_weight[None] * gate_sig * (1.0 + pre_act * (1.0 - gate_sig))
    )
    hidden_bf = hidden_grad.astype(jnp.bfloat16)
    weight_grad = jnp.einsum("rkm,ri->kmi", hidden_bf, lagged, preferred_element_type=jnp.float32)
    grad_trans = (weight_grad * edge_prob[:, None, :]).astype(jnp.bfloat16)
    flip = edge_prob * (1.0 - edge_prob)
    grad_graph = (
        jnp.sum(weight_grad * trans_weight.astype(jnp.float32), axis=1) * flip
        + sparsity_weight * flip
    )
    input_grad = jnp.einsum(
        "rkm,kmi->ri", hidden_bf, eff_weight, preferred_element_type=jnp.float32
    )
    input_grad = input_grad.reshape(batch_size, step_count - LAGS, LAGS, latent_count)
    owned_terms = lax.psum_scatter(input_grad, ("space", "lat"), scatter_dimension=3, tiled=True)
    lag_grad = jnp.zeros((batch_size, step_count, lat_dev), jnp.float32)
    for lag in range(1, LAGS + 1):
        lag_grad = lag_grad + jnp.pad(
            owned_terms[:, :, lag - 1, :], ((0, 0), (LAGS - lag, lag), (0, 0))
        )
    grad_above = shifted(window_grad[:, :, :lat_dev], ("space", "lat"), -1)
    grad_below = shifted(window_grad[:, :, 2 * lat_dev :], ("space", "lat"), 1)
    direct_steps = jnp.pad(
        direct.reshape(batch_size, step_count - LAGS, lat_dev), ((0, 0), (LAGS, 0), (0, 0))
    )
    own_grad = (
        window_grad[:, :, lat_dev : 2 * lat_dev] + grad_above + grad_below + lag_grad + direct_steps
    )
    halo_grad = extended(own_grad, ((("space", "lat"), 2),), lat_dev)
    cell_total = jnp.einsum("btj,cj->btc", halo_grad, one_hot, precision=highest)
    grad_enc = jnp.einsum("btvc,btc->vc", fields.astype(jnp.float32), cell_total, precision=highest)
    return (grad_enc, grad_dec, grad_trans, grad_graph)


def solution(mesh):
    return jax.shard_map(
        body,
        mesh=mesh,
        in_specs=(
            P(None, None, None, ("space", "lat")),
            P(("space", "lat")),
            P(None, ("space", "lat")),
            P(None, ("space", "lat")),
            P(("space", "lat"), None, None),
            P(("space", "lat"), None),
            P(("space", "lat"), None),
            P(("space", "lat"), None),
            P(("space", "lat")),
        ),
        out_specs=(
            P(None, ("space", "lat")),
            P(None, ("space", "lat")),
            P(("space", "lat"), None, None),
            P(("space", "lat"), None),
        ),
        check_vma=False,
    )
```

profile of v0, /device:TPU:1, one launch (start us, length us, event | category | flops | bytes accessed | tf_op | source)
XLA Modules:
  0.0 460.4 jit_solution(15953483216375521314)
XLA Ops:
  7.9 2.8 fusion.9
  14.7 131.0 %all-reduce.11.cloned.1.call-done = f32[4,64,1024]{2,1,0:T(8,128)} async-done(((f32[4,64,1024]{2,1,0:T(8,128)}), f32[4,64,1024]{2,1,0:T(8,128)}) %all-reduce.11.cloned.1.call-update) | async-done | bytes 1048592 | tf_op jit(solution)/shard_map/psum | solution.py:55
  151.0 3.1 collective-permute-start.1
  154.1 3.3 collective-permute-start
  157.9 3.4 copy.19
  161.3 6.8 %reshape.55 = bf16[236,5120,1]{1,0,2:T(8,128)(2,1)} reshape(bf16[4,59,5,1024]{3,2,1,0:T(8,128)(2,1)} %copy.19) | data formatting | bytes 4833280 | tf_op jit(solution)/shard_map/reshape | solution.py:68
  168.1 12.6 %multiply_reduce_fusion.3 = (f32[236,32]{0,1:T(8,128)}, f32[236,32,64]{0,2,1:T(8,128)}) fusion(f32[32,64]{1,0:T(8,128)} %param.16, f32[32,64]{1,0:T(8,128)} %param.15, bf16[236,5120,1]{1,0,2:T(8,128)(2,1)} %reshape.55, bf16[32,64,5120]{2,1,0:T(8,128)(2,1)} %param.13, f32[32,5120]{1,0:T(8,128)S(1)} %add_divide_fusion.1), kind=kOutput, calls=%fused_computation.16 | convolution fusion | flops 4984111616 | bytes 26023424 | tf_op jit(solution)/shard_map/ri,kmi->rkm/dot_general | solution.py:72
  182.1 1.6 copy.26
  183.8 1.8 multiply_divide_fusion
  185.5 1.6 copy.18
  190.2 16.1 %fusion.6 = f32[236,5120]{1,0:T(8,128)} fusion(bf16[32,64,5120]{2,1,0:T(8,128)(2,1)} %param.13, f32[32,5120]{1,0:T(8,128)S(1)} %add_divide_fusion.1, f32[236,32,64]{0,2,1:T(8,128)} %get-tuple-element.18, f32[236,32]{0,1:T(8,128)} %divide_negate_fusion, f32[32,64]{1,0:T(8,128)} %param.16, f32[32,64]{1,0:T(8,128)} %param.15), kind=kOutput, calls=%fused_computation.9 | convolution fusion | flops 4986052608 | bytes 28440064 | tf_op jit(solution)/shard_map/rkm,kmi->ri/dot_general | solution.py:90
  206.3 7.5 %reshape.53 = f32[4,59,5,1024]{3,2,1,0:T(8,128)} reshape(f32[236,5120]{1,0:T(8,128)} %fusion.6) | data formatting | bytes 9666560 | tf_op jit(solution)/shard_map/reshape | solution.py:93
  213.8 10.4 %copy.20 = f32[4,59,5,1024]{1,0,2,3:T(4,128)} copy(f32[4,59,5,1024]{3,2,1,0:T(8,128)} %reshape.53) | data formatting | bytes 9666560 | tf_op jit(solution)/shard_map/reshape | solution.py:93
  224.2 23.0 %fusion.1 = (f32[32,5120]{1,0:T(8,128)}, bf16[32,64,5120]{2,1,0:T(8,128)(2,1)}) fusion(bf16[32,64,5120]{2,1,0:T(8,128)(2,1)} %param.13, f32[32,5120]{1,0:T(8,128)S(1)} %add_divide_fusion.1, bf16[236,5120,1]{1,0,2:T(8,128)(2,1)} %reshape.55, f32[236,32,64]{0,2,1:T(8,128)} %get-tuple-element.18, f32[236,32]{0,1:T(8,128)} %divide_negate_fusion, ...), kind=kOutput, calls=%fused_computation.3 | convolution fusion | flops 5006860288 | bytes 47650304 | tf_op jit(solution)/shard_map/rkm,ri->kmi/dot_general | solution.py:83
  247.2 179.6 %all-reduce.13.cloned.1.call-done = f32[4,59,5,1024]{1,0,2,3:T(4,128)} async-done(((f32[4,59,5,1024]{1,0,2,3:T(4,128)}), f32[4,59,5,1024]{1,0,2,3:T(4,128)}) %all-reduce.13.cloned.1.call-update) | async-done | bytes 4833296
  426.8 1.7 constant_dynamic-slice_fusion.3
  430.1 1.6 copy.44
  431.8 1.6 copy.43
  433.4 1.6 copy.42
  435.0 1.6 copy.41
  438.0 4.0 collective-permute-start.3
  442.0 1.9 collective-permute-start.2
  445.0 4.7 %collective-permute-done.2 = f32[4,64,32]{2,1,0:T(8,128)S(1)} collective-permute-done((f32[4,64,32]{2,1,0:T(8,128)S(1)}, f32[4,64,32]{2,1,0:T(8,128)S(1)}, u32[]{:S(2)}, u32[]{:S(2)}) %collective-permute-start.2) | collective-permute-done | bytes 32800 | tf_op jit(solution)/shard_map/ppermute | solution.py:21
  450.7 2.2 multiply_reduce_fusion
  (45 shorter events, 20.6 us)
Async XLA Ops:
  7.2 138.6 %all-reduce.11.cloned.1.call-start = ((), (), s32[]{:S(2)}) async-start(), calls=%async_computation | async-start | bytes 2097152 | tf_op jit(solution)/shard_map/psum | solution.py:55
  11.9 2.6 copy-start.2
  14.5 412.4 %all-reduce.13.cloned.1.call-start = ((), (), s32[]{:S(2)}) async-start(), calls=%async_computation.1 | async-start | bytes 20971520
  14.7 133.1 %copy-start.4 = (f32[3,2048]{1,0:T(4,128)S(1)}, f32[3,2048]{1,0:T(4,128)}, u32[]{:S(2)}) copy-start(f32[3,2048]{1,0:T(4,128)} %param.12) | copy-start | bytes 73732
  145.7 2.2 copy-start
  151.0 285.5 %collective-permute-start.1 = (f32[4,64,32]{2,1,0:T(8,128)}, f32[4,64,32]{2,1,0:T(8,128)}, u32[]{:S(2)}, u32[]{:S(2)}) collective-permute-start(f32[4,64,32]{2,1,0:T(8,128)} %get-tuple-element.16), channel_id=1, source_target_pairs={{0,1},{1,2},{2,3},{3,4},{4,5},{5,6},{6,7},{7,8},{8,9},{9,10},{10,1... | collective-permute-start | bytes 98312 | tf_op jit(solution)/shard_map/ppermute | solution.py:13
  154.1 282.5 %collective-permute-start = (f32[4,64,32]{2,1,0:T(8,128)}, f32[4,64,32]{2,1,0:T(8,128)}, u32[]{:S(2)}, u32[]{:S(2)}) collective-permute-start(f32[4,64,32]{2,1,0:T(8,128)} %get-tuple-element.15), channel_id=1, source_target_pairs={{1,0},{2,1},{3,2},{4,3},{5,4},{6,5},{7,6},{8,7},{9,8},{10,9},{11,1... | collective-permute-start | bytes 98312 | tf_op jit(solution)/shard_map/ppermute | solution.py:13
  168.1 15.7 %copy-start.6 = (f32[32]{0:T(128)S(1)}, f32[32]{0:T(128)}, u32[]{:S(2)}) copy-start(f32[32]{0:T(128)} %param.17) | copy-start | bytes 388
  247.2 196.8 %copy-start.3 = (f32[32,5120]{1,0:T(8,128)S(1)}, f32[32,5120]{1,0:T(8,128)}, u32[]{:S(2)}) copy-start(f32[32,5120]{1,0:T(8,128)} %get-tuple-element.8) | copy-start | bytes 1966084
  438.0 12.7 %copy-start.1 = (bf16[4,64,3,2048]{3,1,2,0:T(8,128)(2,1)S(1)}, bf16[4,64,3,2048]{3,1,2,0:T(8,128)(2,1)}, u32[]{:S(2)}) copy-start(bf16[4,64,3,2048]{3,1,2,0:T(8,128)(2,1)} %param.9) | copy-start | bytes 9437188
  438.0 12.7 %copy-start.5 = (f32[3,2048]{1,0:T(4,128)S(1)}, f32[3,2048]{1,0:T(4,128)}, u32[]{:S(2)}) copy-start(f32[3,2048]{1,0:T(4,128)} %param.12) | copy-start | bytes 73732
  438.0 7.0 %collective-permute-start.3 = (f32[4,64,32]{2,1,0:T(8,128)S(1)}, f32[4,64,32]{2,1,0:T(8,128)S(1)}, u32[]{:S(2)}, u32[]{:S(2)}) collective-permute-start(f32[4,64,32]{2,1,0:T(8,128)S(1)} %fusion.32), channel_id=1, source_target_pairs={{1,0},{2,1},{3,2},{4,3},{5,4},{6,5},{7,6},{8,7},{9,8},{10,9},{11,1... | collective-permute-start | bytes 98312 | tf_op jit(solution)/shard_map/ppermute | solution.py:24
  442.0 7.6 %collective-permute-start.2 = (f32[4,64,32]{2,1,0:T(8,128)S(1)}, f32[4,64,32]{2,1,0:T(8,128)S(1)}, u32[]{:S(2)}, u32[]{:S(2)}) collective-permute-start(f32[4,64,32]{2,1,0:T(8,128)S(1)} %fusion.32), channel_id=1, source_target_pairs={{0,1},{1,2},{2,3},{3,4},{4,5},{5,6},{6,7},{7,8},{8,9},{9,10},{10,1... | collective-permute-start | bytes 98312 | tf_op jit(solution)/shard_map/ppermute | solution.py:21
Sparse Core Ops, SparseCore 0:
  14.6 131.1 all-reduce.10
  224.4 202.4 all-reduce.12
where the time goes:
time: 462 us; the launch traced here: 460 us
  waiting for transfers between devices  315 us (68%)
  matrix products  55.6 us (12%)
  local copies, waits for them, and re-layouts  48 us (10%)
  other arithmetic  14.7 us (3%)
  between operations  14.3 us (3%)
  starting transfers between devices  12.4 us (3%)
    unnamed x3, waiting for transfers between devices  180 us
    psum x1, waiting for transfers between devices, body(): lax.psum(spread_table[:, :, lat_dev:latent_count + lat_dev], ('space', 'l...  131 us
    dot_general x1, matrix products, body(): jnp.einsum('rkm,ri->kmi', hidden_bf, lagged, preferred_element_type=jnp.f...  23 us
    reshape x2, local copies, waits for them, and re-layouts, body(): input_grad.reshape(batch_size, step_count - LAGS, LAGS, latent_count)  17.9 us
    dot_general x1, matrix products, body(): jnp.einsum('rkm,kmi->ri', hidden_bf, eff_weight, preferred_element_type=j...  16.1 us
    dot_general x1, matrix products, body(): jnp.einsum('ri,kmi->rkm', lagged, eff_weight, preferred_element_type=jnp....  12.6 us
  transfers between devices with their start and end apart: 6, of which 3 were waited for; matrix products, arithmetic and copies ran while one was open for 22% of the time, Pallas kernels for 0%

commit v1 on v0

--- a/solution.py
+++ b/solution.py
@@ -1,3 +1,4 @@
+import functools
 import jax
 import jax.numpy as jnp
 from jax import lax
@@ -5,6 +6,14 @@
 
 LAGS = 5
 sparsity_weight = 0.01
+
+
+def draft_target_here(u_in, axis_id):
+    odd = jnp.sum(jax.lax.all_gather(u_in, axis_id), 0)
+    return odd
+
+
+measure_routes_all_over_axis = functools.partial(draft_target_here, axis_id=("space", "lat"))
 
 
 def shifted(block, axis, distance):
@@ -52,7 +61,7 @@
     enc_part = jnp.einsum("btc,cj->btj", projected, one_hot, precision=highest)
     spread_table = jnp.zeros((batch_size, step_count, latent_count + 2 * lat_dev), jnp.float32)
     spread_table = lax.dynamic_update_slice_in_dim(spread_table, enc_part, device * lat_dev, 2)
-    latent_full = lax.psum(spread_table[:, :, lat_dev : latent_count + lat_dev], ("space", "lat"))
+    latent_full = measure_routes_all_over_axis(spread_table[:, :, lat_dev : latent_count + lat_dev])
     own_latent = lax.dynamic_slice_in_dim(latent_full, device * lat_dev, lat_dev, 2)
     latent_bf = latent_full.astype(jnp.bfloat16)
     padded_latent = jnp.pad(latent_bf, ((0, 0), (0, 0), (lat_dev, lat_dev)))

time: 462 us -> 525 us (1.14)
  waiting for transfers between devices: 315 us -> 377 us
  other arithmetic: 14.7 us -> 25.3 us
  local copies, waits for them, and re-layouts: 48 us -> 40.4 us
    all_gather x0 -> x1, waiting for transfers between devices: none -> 196 us  [draft_target_here(): odd = jnp.sum(jax.lax.all_gather(u_in, axis_id), 0)]
    psum x1 -> x0, waiting for transfers between devices: 131 us -> none  [body(): lax.psum(spread_table[:, :, lat_dev:latent_count + lat_dev], ('space', 'l...]
    reduce_sum x0 -> x1, other arithmetic: none -> 11.9 us  [draft_target_here(): odd = jnp.sum(jax.lax.all_gather(u_in, axis_id), 0)]
  transfers between devices with their start and end apart: 6 -> 6, of which waited for: 3 -> 3; matrix products, arithmetic and copies ran while one was open for 22% -> 17% of each run, Pallas kernels for 0% -> 0%
where the time goes in v1:
time: 525 us; the launch traced here: 524 us
  waiting for transfers between devices  377 us (72%)
  matrix products  55.4 us (11%)
  local copies, waits for them, and re-layouts  40.4 us (8%)
  other arithmetic  25.3 us (5%)
  between operations  14.3 us (3%)
  starting transfers between devices  11.6 us (2%)
    all_gather x1, waiting for transfers between devices, draft_target_here(): odd = jnp.sum(jax.lax.all_gather(u_in, axis_id), 0)  196 us
    unnamed x3, waiting for transfers between devices  177 us
    dot_general x1, matrix products, body(): jnp.einsum('rkm,ri->kmi', hidden_bf, lagged, preferred_element_type=jnp.f...  23.3 us
    reshape x2, local copies, waits for them, and re-layouts, body(): input_grad.reshape(batch_size, step_count - LAGS, LAGS, latent_count)  17.9 us
    dot_general x1, matrix products, body(): jnp.einsum('rkm,kmi->ri', hidden_bf, eff_weight, preferred_element_type=j...  16.2 us
    dot_general x1, matrix products, body(): jnp.einsum('ri,kmi->rkm', lagged, eff_weight, preferred_element_type=jnp....  12 us
    reduce_sum x1, other arithmetic, draft_target_here(): odd = jnp.sum(jax.lax.all_gather(u_in, axis_id), 0)  11.9 us
  transfers between devices with their start and end apart: 6, of which 3 were waited for; matrix products, arithmetic and copies ran while one was open for 17% of the time, Pallas kernels for 0%

profile of v1, /device:TPU:1, one launch (start us, length us, event | category | flops | bytes accessed | tf_op | source)
XLA Modules:
  0.0 524.0 jit_solution(13015529915717454145)
XLA Ops:
  7.9 2.8 fusion.9
  10.7 1.2 fusion.18
  13.1 1.3 slice.60
  15.5 196.4 %all-gather.3.cloned.1.call-done = f32[128,64,1024]{2,1,0:T(8,128)} async-done(((f32[4,64,1024]{2,1,0:T(8,128)}), f32[128,64,1024]{2,1,0:T(8,128)}) %all-gather.3.cloned.1.call-update) | async-done | bytes 33554448 | tf_op jit(solution)/shard_map/all_gather | solution.py:12
  211.9 11.9 %reduce_sum.48 = f32[4,64,1024]{2,1,0:T(8,128)S(1)} reduce(f32[32,4,64,1024]{3,2,1,0:T(8,128)} %bitcast.51, f32[]{:T(128)} %constant.13.clone.1), dimensions={0}, to_apply=%region_1.0 | reduce | flops 8126464 | bytes 34603012 | tf_op jit(solution)/shard_map/reduce_sum | solution.py:12
  224.5 1.1 copy-done
  226.8 1.2 fusion.10
  228.8 3.0 collective-permute-start.1
  231.8 2.5 collective-permute-start
  234.8 3.4 copy.19
  238.2 6.7 %reshape.56 = bf16[236,5120,1]{1,0,2:T(8,128)(2,1)} reshape(bf16[4,59,5,1024]{3,2,1,0:T(8,128)(2,1)} %copy.19) | data formatting | bytes 4833280 | tf_op jit(solution)/shard_map/reshape | solution.py:77
  245.0 12.0 %multiply_reduce_fusion.3 = (f32[236,32]{0,1:T(8,128)S(1)}, f32[236,32,64]{0,2,1:T(8,128)}) fusion(f32[32,64]{1,0:T(8,128)S(1)} %copy-done.9, f32[32,64]{1,0:T(8,128)S(1)} %copy-done.11, bf16[236,5120,1]{1,0,2:T(8,128)(2,1)} %reshape.56, bf16[32,64,5120]{2,1,0:T(8,128)(2,1)} %param.13, f32[32,5120]{1,0:T(8,128)} %add_divide_fusion.1), kind=kOutput, calls=%fused_computation.16 | convolution fusion | flops 4984111616 | bytes 26023424 | tf_op jit(solution)/shard_map/ri,kmi->rkm/dot_general | solution.py:81
  260.5 16.2 %fusion.6 = f32[236,5120]{1,0:T(8,128)} fusion(bf16[32,64,5120]{2,1,0:T(8,128)(2,1)} %param.13, f32[32,5120]{1,0:T(8,128)} %add_divide_fusion.1, f32[236,32,64]{0,2,1:T(8,128)} %get-tuple-element.18, f32[236,32]{0,1:T(8,128)S(1)} %divide_negate_fusion, f32[32,64]{1,0:T(8,128)} %param.16, f32[32,64]{1,0:T(8,128)} %param.15), kind=kOutput, calls=%fused_computation.9 | convolution fusion | flops 4986052608 | bytes 28440064 | tf_op jit(solution)/shard_map/rkm,kmi->ri/dot_general | solution.py:99
  276.6 7.5 %reshape.53 = f32[4,59,5,1024]{3,2,1,0:T(8,128)} reshape(f32[236,5120]{1,0:T(8,128)} %fusion.6) | data formatting | bytes 9666560 | tf_op jit(solution)/shard_map/reshape | solution.py:102
  284.2 10.4 %copy.20 = f32[4,59,5,1024]{1,0,2,3:T(4,128)} copy(f32[4,59,5,1024]{3,2,1,0:T(8,128)} %reshape.53) | data formatting | bytes 9666560 | tf_op jit(solution)/shard_map/reshape | solution.py:102
  295.6 23.3 %fusion.1 = (f32[32,5120]{1,0:T(8,128)}, bf16[32,64,5120]{2,1,0:T(8,128)(2,1)}) fusion(bf16[32,64,5120]{2,1,0:T(8,128)(2,1)} %param.13, f32[32,5120]{1,0:T(8,128)S(1)} %copy-done.4, bf16[236,5120,1]{1,0,2:T(8,128)(2,1)} %reshape.56, f32[236,32,64]{0,2,1:T(8,128)} %get-tuple-element.18, f32[236,32]{0,1:T(8,128)S(1)} %divide_negate_fusion, ...), kind=kOutput, calls=%fused_computation.3 | convolution fusion | flops 5006860288 | bytes 47650304 | tf_op jit(solution)/shard_map/rkm,ri->kmi/dot_general | solution.py:92
  319.0 177.0 %all-reduce.10.cloned.1.call-done = f32[4,59,5,1024]{1,0,2,3:T(4,128)} async-done(((f32[4,59,5,1024]{1,0,2,3:T(4,128)}), f32[4,59,5,1024]{1,0,2,3:T(4,128)}) %all-reduce.10.cloned.1.call-update) | async-done | bytes 4833296
  496.0 1.6 constant_dynamic-slice_fusion.3
  500.4 1.2 fusion.32
  501.6 4.0 collective-permute-start.3
  505.7 1.9 collective-permute-start.2
  507.6 2.1 fusion.20
  509.7 3.6 collective-permute-done.2
  514.4 2.2 multiply_reduce_fusion
  (58 shorter events, 15.0 us)
Async XLA Ops:
  7.2 204.8 %all-gather.3.cloned.1.call-start = ((), (), s32[]{:S(2)}) async-start(), calls=%async_computation | async-start | bytes 34603008 | tf_op jit(solution)/shard_map/all_gather | solution.py:12
  11.9 2.6 copy-start.2
  14.5 481.6 %all-reduce.10.cloned.1.call-start = ((), (), s32[]{:S(2)}) async-start(), calls=%async_computation.1 | async-start | bytes 20971520
  223.8 1.9 copy-start
  223.8 1.9 copy-start.5
  228.8 271.6 %collective-permute-start.1 = (f32[4,64,32]{2,1,0:T(8,128)}, f32[4,64,32]{2,1,0:T(8,128)}, u32[]{:S(2)}, u32[]{:S(2)}) collective-permute-start(f32[4,64,32]{2,1,0:T(8,128)} %get-tuple-element.16), channel_id=1, source_target_pairs={{0,1},{1,2},{2,3},{3,4},{4,5},{5,6},{6,7},{7,8},{8,9},{9,10},{10,1... | collective-permute-start | bytes 98312 | tf_op jit(solution)/shard_map/ppermute | solution.py:22
  231.8 268.6 %collective-permute-start = (f32[4,64,32]{2,1,0:T(8,128)}, f32[4,64,32]{2,1,0:T(8,128)}, u32[]{:S(2)}, u32[]{:S(2)}) collective-permute-start(f32[4,64,32]{2,1,0:T(8,128)} %get-tuple-element.15), channel_id=1, source_target_pairs={{1,0},{2,1},{3,2},{4,3},{5,4},{6,5},{7,6},{8,7},{9,8},{10,9},{11,1... | collective-permute-start | bytes 98312 | tf_op jit(solution)/shard_map/ppermute | solution.py:22
  238.2 6.8 %copy-start.9 = (f32[32,64]{1,0:T(8,128)S(1)}, f32[32,64]{1,0:T(8,128)}, u32[]{:S(2)}) copy-start(f32[32,64]{1,0:T(8,128)} %param.16) | copy-start | bytes 24580
  238.2 6.8 %copy-start.11 = (f32[32,64]{1,0:T(8,128)S(1)}, f32[32,64]{1,0:T(8,128)}, u32[]{:S(2)}) copy-start(f32[32,64]{1,0:T(8,128)} %param.15) | copy-start | bytes 24580
  245.0 12.8 %copy-start.8 = (f32[32]{0:T(128)S(1)}, f32[32]{0:T(128)}, u32[]{:S(2)}) copy-start(f32[32]{0:T(128)} %param.17) | copy-start | bytes 388
  257.0 0.6 copy-start.7
  294.6 1.1 copy-start.4
  294.6 1.1 copy-start.10
  294.6 1.1 copy-start.12
  319.0 188.6 %copy-start.3 = (f32[32,5120]{1,0:T(8,128)S(1)}, f32[32,5120]{1,0:T(8,128)}, u32[]{:S(2)}) copy-start(f32[32,5120]{1,0:T(8,128)} %param.14) | copy-start | bytes 1966084
  501.6 12.7 %copy-start.1 = (bf16[4,64,3,2048]{3,1,2,0:T(8,128)(2,1)S(1)}, bf16[4,64,3,2048]{3,1,2,0:T(8,128)(2,1)}, u32[]{:S(2)}) copy-start(bf16[4,64,3,2048]{3,1,2,0:T(8,128)(2,1)} %param.9) | copy-start | bytes 9437188
  501.6 12.7 %copy-start.6 = (f32[3,2048]{1,0:T(4,128)S(1)}, f32[3,2048]{1,0:T(4,128)}, u32[]{:S(2)}) copy-start(f32[3,2048]{1,0:T(4,128)} %param.12) | copy-start | bytes 73732
  501.6 8.1 %collective-permute-start.3 = (f32[4,64,32]{2,1,0:T(8,128)S(1)}, f32[4,64,32]{2,1,0:T(8,128)S(1)}, u32[]{:S(2)}, u32[]{:S(2)}) collective-permute-start(f32[4,64,32]{2,1,0:T(8,128)S(1)} %fusion.32), channel_id=1, source_target_pairs={{1,0},{2,1},{3,2},{4,3},{5,4},{6,5},{7,6},{8,7},{9,8},{10,9},{11,1... | collective-permute-start | bytes 98312 | tf_op jit(solution)/shard_map/ppermute | solution.py:33
  505.7 7.6 %collective-permute-start.2 = (f32[4,64,32]{2,1,0:T(8,128)S(1)}, f32[4,64,32]{2,1,0:T(8,128)S(1)}, u32[]{:S(2)}, u32[]{:S(2)}) collective-permute-start(f32[4,64,32]{2,1,0:T(8,128)S(1)} %fusion.32), channel_id=1, source_target_pairs={{0,1},{1,2},{2,3},{3,4},{4,5},{5,6},{6,7},{7,8},{8,9},{9,10},{10,1... | collective-permute-start | bytes 98312 | tf_op jit(solution)/shard_map/ppermute | solution.py:30
Sparse Core Ops, SparseCore 0:
  14.6 197.2 all-gather.2
  294.7 201.2 all-reduce.9
